TPU v7x, 128 devices: a whole 4x4x4 slice. The times are simulated.
128 devices in a mesh: enc: 8 (over z, core), ctx: 16 (over y, x).
Axes of the slice: x: 4, y: 4, z: 4, core: 2. Of those that a mesh axis runs over, the one named last changes fastest.
Arguments:
- patches: bfloat16 [6144, 1280], P('enc'), may hold values from -17 to 17
- patch_image: int32 [6144], P('enc'), may hold values from 63 to 1535, as said below
- vit_gain: float32 [1280], replicated, may hold values from 0.1 to 1.9
- vit_qkv: bfloat16 [1280, 16, 240], P(None, 'ctx')
- vit_proj: bfloat16 [1280, 1280], P('ctx'), may hold values from -0.15625 to 0.15625
- merge_gain: float32 [1280], replicated, may hold values from 0.1 to 1.9
- merge_up: bfloat16 [5120, 5120], P(None, 'ctx'), may hold values from -0.078125 to 0.078125
- merge_down: bfloat16 [5120, 8192], P('ctx', 'enc'), may hold values from -0.078125 to 0.078125
- text_embed: bfloat16 [6144, 8192], P('ctx', 'enc'), may hold values from -17 to 17
- placeholder_unit: int32 [6144], replicated, may hold values from -1 to 1535, as said below
- doc_id: int32 [6144], replicated, may hold values from 0 to 31, never falling along the last dimension, each value on 1 to 3456 neighbouring positions
- dec_gain: float32 [8192], replicated, may hold values from 0.1 to 1.9
- dec_wq: bfloat16 [8192, 4096], P(None, 'enc')
- dec_wk: bfloat16 [8192, 1024], P(None, 'enc')
- dec_wv: bfloat16 [8192, 1024], P(None, 'enc'), may hold values from -0.0625 to 0.0625
Outputs:
- attended: bfloat16 [6144, 4096], P('ctx', 'enc')
Inputs may be any that keep to these rules, and one draw needn't show every extreme that they name: `patch_image`: the patches of an image are consecutive, start at a multiple of 4, number a multiple of 4 and at most 256, and lie within one aligned block of 768 patches; image numbers never fall and differ between images; in every such block some image has exactly 256 patches. `placeholder_unit`: -1 marks a text position. Every unit appears exactly once; the units of one image fill consecutive placeholders in their order; the placeholders of an aligned block of 384 positions are consecutive and number at most 192, and some block holds exactly 192. `doc_id`: document numbers never fall; a document has at most 3456 positions, and some document exactly 3456.
All inputs are finite; a program needn't handle non-finite values.
Results may differ from a plain program's by a relative error of at most 0.0085.
Values may be sent and summed in bfloat16 or wider, within the bound.
A program may use at most 128 MiB of HBM per device.

v0:
```python
import math
import jax
import jax.numpy as jnp
from jax import lax
from jax.sharding import PartitionSpec as P

HD = 128
QPK = 4
EPSILON = 1e-06
NEGATIVE = -1e30


def in_blocks(x, dim, size):
    dims = x.shape
    blocks = x.reshape(*dims[:dim], size, dims[dim] // size, *dims[dim + 1 :])
    return jnp.moveaxis(blocks, dim, 0)


def sent_and_summed(x, axis, dim):
    blocks = in_blocks(x, dim, lax.axis_size(axis))
    arrived = lax.all_to_all(blocks, axis, split_axis=0, concat_axis=0, tiled=True)
    return arrived.sum(axis=0)


def in_order(blocks, dim):
    dims = list(blocks.shape[1:])
    dims[dim] *= blocks.shape[0]
    return jnp.moveaxis(blocks, 0, dim).reshape(dims)


def sent_to_all(x, axis):
    size = lax.axis_size(axis)
    return lax.all_to_all(jnp.broadcast_to(x[None], (size, *x.shape)), axis, 0, 0, tiled=True)


def gathered_copies(x, axis, dim):
    return in_order(sent_to_all(x, axis), dim)


def of_everyone(x, axis):
    return sent_to_all(x, axis).sum(axis=0)


def in_one_piece(arrays, axis, dim, along):
    widths = [a.shape[along] for a in arrays]
    both = jnp.concatenate(arrays, axis=along)
    result = lax.all_gather(both, axis, axis=dim, tiled=True)
    return tuple(jnp.split(result, [sum(widths[:k]) for k in range(1, len(widths))], axis=along))


def layer_norm(values, scaling):
    widened = values.astype(jnp.float32)
    center = widened - jnp.mean(widened, axis=1, keepdims=True)
    spread = jnp.mean(center * center, axis=1, keepdims=True)
    return (center * lax.rsqrt(spread + EPSILON) * scaling).astype(jnp.bfloat16)


def image_attention(queries, keys_in, values_in, image_ids):
    head_count, row_count, head_width = queries.shape
    block_rows = math.gcd(row_count, 512)
    scaling = head_width ** (-0.5)

    def image_one_block(offset):
        query_block = lax.dynamic_slice_in_dim(queries, offset, block_rows, 1)
        block_ids = lax.dynamic_slice_in_dim(image_ids, offset, block_rows, 0)
        allowed = block_ids[:, None] == image_ids[None, :]
        scores = (
            jnp.einsum("hqd,hkd->hqk", query_block, keys_in, preferred_element_type=jnp.float32)
            * scaling
        )
        scores = jnp.where(allowed[None], scores, NEGATIVE)
        highest = jnp.max(scores, axis=2, keepdims=True)
        weights = jnp.exp(scores - highest)
        totals = jnp.sum(weights, axis=2, keepdims=True)
        mixture = jnp.einsum(
            "hqk,hkd->hqd",
            weights.astype(jnp.bfloat16),
            values_in,
            preferred_element_type=jnp.float32,
        )
        return (mixture / totals).astype(jnp.bfloat16)

    offsets = jnp.arange(row_count // block_rows, dtype=jnp.int32) * block_rows
    blocks = lax.map(image_one_block, offsets)
    return blocks.transpose(1, 0, 2, 3).reshape(head_count, row_count, head_width)


def body(
    patches,
    patch_image,
    vit_gain,
    vit_qkv,
    vit_proj,
    merge_gain,
    merge_up,
    merge_down,
    text_embed,
    placeholder_unit,
    doc_id,
    dec_gain,
    dec_wq,
    dec_wk,
    dec_wv,
):
    ctx_count = lax.axis_size("ctx")
    enc_count = lax.axis_size("enc")
    ctx_index = lax.axis_index("ctx")
    group_rows = patches.shape[0]
    head_count = vit_qkv.shape[1]
    head_width = vit_qkv.shape[2] // 3
    normed_patches = layer_norm(patches, vit_gain)
    packed = jnp.dot(
        normed_patches,
        vit_qkv.reshape(vit_qkv.shape[0], head_count * 3 * head_width),
        preferred_element_type=jnp.float32,
    )
    packed = (
        packed.astype(jnp.bfloat16)
        .reshape(group_rows, head_count, 3, head_width)
        .transpose(2, 1, 0, 3)
    )
    attended_patches = image_attention(packed[0], packed[1], packed[2], patch_image)
    flat_heads = attended_patches.transpose(1, 0, 2).reshape(group_rows, head_count * head_width)
    head_terms = jnp.dot(flat_heads, vit_proj, preferred_element_type=jnp.float32)
    share_sum = sent_and_summed(head_terms, "ctx", 0)
    share_count = share_sum.shape[0]
    own_rows = lax.dynamic_slice_in_dim(patches, ctx_index * share_count, share_count, 0)
    own_out = (own_rows.astype(jnp.float32) + share_sum).astype(jnp.bfloat16)
    own_normed = layer_norm(lax.optimization_barrier(own_out), merge_gain)
    merge_input = gathered_copies(own_normed, "ctx", 0)
    unit_inputs = merge_input.reshape(group_rows // 4, 4 * merge_input.shape[1])
    hidden = jax.nn.gelu(
        jnp.dot(unit_inputs, merge_up, preferred_element_type=jnp.float32), approximate=False
    ).astype(jnp.bfloat16)
    all_hidden = gathered_copies(hidden, "enc", 0)
    unit_total = all_hidden.shape[0]
    tok_rows = text_embed.shape[0]
    feature_cols = text_embed.shape[1]
    local_units = lax.dynamic_slice_in_dim(placeholder_unit, ctx_index * tok_rows, tok_rows, 0)
    present = local_units >= 0
    slot_rows = tok_rows // 2
    shard_units = placeholder_unit.reshape(ctx_count, tok_rows)
    shard_present = shard_units >= 0
    shard_rank = jnp.cumsum(shard_present.astype(jnp.int32), axis=1) - 1
    matches = shard_present[:, None, :] & (
        shard_rank[:, None, :] == jnp.arange(slot_rows, dtype=jnp.int32)[None, :, None]
    )
    slot_units = (jnp.sum(jnp.where(matches, shard_units[:, None, :] + 1, 0), axis=2) - 1).reshape(
        -1
    )
    picked = jnp.take(all_hidden, jnp.clip(slot_units, 0, unit_total - 1), axis=0)
    picked = jnp.where((slot_units >= 0)[:, None], picked, jnp.zeros_like(picked))
    arrived = lax.psum_scatter(
        jnp.dot(picked, merge_down, preferred_element_type=jnp.float32),
        "ctx",
        scatter_dimension=0,
        tiled=True,
    ).astype(jnp.bfloat16)
    local_rank = jnp.cumsum(present.astype(jnp.int32)) - 1
    vision_local = jnp.take(arrived, jnp.clip(local_rank, 0, slot_rows - 1), axis=0)
    sequence = jnp.where(present[:, None], vision_local, text_embed)
    local_wide = sequence.astype(jnp.float32)
    squares = of_everyone(jnp.sum(local_wide * local_wide, axis=1), "enc")
    row_scale = lax.rsqrt(squares / (feature_cols * enc_count) + EPSILON)
    start_state = (
        jnp.zeros((tok_rows, dec_wq.shape[1]), jnp.float32),
        jnp.zeros((tok_rows, dec_wk.shape[1]), jnp.float32),
        jnp.zeros((tok_rows, dec_wv.shape[1]), jnp.float32),
    )
    normed_part = (
        lax.all_gather(sequence, "enc", axis=1, tiled=True).astype(jnp.float32)
        * row_scale[:, None]
        * dec_gain
    ).astype(jnp.bfloat16)
    query_part = jnp.dot(normed_part, dec_wq, preferred_element_type=jnp.float32)
    key_part = jnp.dot(normed_part, dec_wk, preferred_element_type=jnp.float32)
    value_part = jnp.dot(normed_part, dec_wv, preferred_element_type=jnp.float32)
    queries_flat = query_part.astype(jnp.bfloat16)
    keys_local = key_part.astype(jnp.bfloat16)
    values_local = value_part.astype(jnp.bfloat16)
    kv_local = dec_wk.shape[1] // HD
    queries = queries_flat.reshape(tok_rows, kv_local, QPK, HD).transpose(1, 2, 0, 3)
    query_first = ctx_index * tok_rows
    query_pos = query_first + jnp.arange(tok_rows, dtype=jnp.int32)
    query_docs = lax.dynamic_slice_in_dim(doc_id, query_first, tok_rows, 0)
    scaling = HD ** (-0.5)
    start_state = (
        jnp.full((kv_local, QPK, tok_rows), NEGATIVE, jnp.float32),
        jnp.zeros((kv_local, QPK, tok_rows), jnp.float32),
        jnp.zeros((kv_local, QPK, tok_rows, HD), jnp.float32),
    )
    offset = jnp.int32(0)
    key_part, value_part = in_one_piece((keys_local, values_local), "ctx", 0, 1)
    key_count = key_part.shape[0]
    sub_rows = math.gcd(key_count, 512)
    last_doc = lax.dynamic_slice_in_dim(doc_id, offset + key_count - 1, 1, 0)[0]
    visible = (offset <= query_first + tok_rows - 1) & (last_doc >= query_docs[0])

    def update(current):

        def update_one_block(turn_index, inner_state):
            highest, totals, mixture = inner_state
            begin_row = turn_index * sub_rows
            keys_block = lax.dynamic_slice_in_dim(key_part, begin_row, sub_rows, 0).reshape(
                sub_rows, kv_local, HD
            )
            values_block = lax.dynamic_slice_in_dim(value_part, begin_row, sub_rows, 0).reshape(
                sub_rows, kv_local, HD
            )
            key_pos = begin_row + jnp.arange(sub_rows, dtype=jnp.int32)
            key_docs = lax.dynamic_slice_in_dim(doc_id, begin_row, sub_rows, 0)
            allowed = (key_pos[None, :] <= query_pos[:, None]) & (
                key_docs[None, :] == query_docs[:, None]
            )
            scores = (
                jnp.einsum(
                    "gjtd,sgd->gjts", queries, keys_block, preferred_element_type=jnp.float32
                )
                * scaling
            )
            new_peak = jnp.maximum(highest, jnp.max(jnp.where(allowed, scores, NEGATIVE), axis=3))
            factor = jnp.exp(highest - new_peak)
            weights = jnp.where(allowed, jnp.exp(scores - new_peak[..., None]), 0.0)
            totals = totals * factor + jnp.sum(weights, axis=3)
            mixture = mixture * factor[..., None] + jnp.einsum(
                "gjts,sgd->gjtd",
                weights.astype(jnp.bfloat16),
                values_block,
                preferred_element_type=jnp.float32,
            )
            return (new_peak, totals, mixture)

        return lax.fori_loop(0, key_count // sub_rows, update_one_block, current)

    def unchanged(current):
        return current

    finished = lax.cond(visible, update, unchanged, start_state)
    outputs = (finished[2] / finished[1][..., None]).astype(jnp.bfloat16)
    return outputs.transpose(2, 0, 1, 3).reshape(tok_rows, kv_local * QPK * HD)


def solution(mesh):
    placed = (
        P("enc", None),
        P("enc"),
        P(),
        P(None, "ctx", None),
        P("ctx", None),
        P(),
        P(None, "ctx"),
        P("ctx", "enc"),
        P("ctx", "enc"),
        P(),
        P(),
        P(),
        P(None, "enc"),
        P(None, "enc"),
        P(None, "enc"),
    )
    return jax.shard_map(
        body, mesh=mesh, in_specs=placed, out_specs=P("ctx", "enc"), check_vma=False
    )
```

profile of v0, /device:TPU:0, one launch (start us, length us, event | category | flops | bytes accessed | tf_op | source)
XLA Modules:
  0.0 493.8 jit_solution(5505292122462072174)
XLA Ops:
  15.2 16.2 %while.28 = (s32[]{:T(128)}, bf16[3,1,256,80]{2,3,1,0:T(8,128)(2,1)}, s32[3]{0:T(128)S(1)}, s32[768]{0:T(1024)S(1)}, bf16[1,768,80]{2,1,0:T(8,128)(2,1)}, /*inde...) while((s32[]{:T(128)}, ...), condition=%wide.region_10.11_spmd, body=%wide.region_7.10_spmd.sunk | while | flops 64527876 | bytes 2797211 | solution.py:84
  32.5 3.5 fusion.79
  36.0 7.2 %all-to-all-start = ((f32[16,48,1280]{2,1,0:T(8,128)}), f32[16,48,1280]{2,1,0:T(8,128)}, u32[]{:S(2)}, u32[]{:S(2)}) async-start(f32[16,48,1280]{2,1,0:T(8,128)} %fusion.79), calls=%async_computation | async-start | bytes 7864320 | tf_op jit(solution)/shard_map/all_to_all | solution.py:21
  43.2 59.5 %all-to-all-done = f32[16,48,1280]{2,1,0:T(8,128)} async-done(((f32[16,48,1280]{2,1,0:T(8,128)}), f32[16,48,1280]{2,1,0:T(8,128)}, u32[]{:S(2)}, u32[]{:S(2)}) %all-to-all-start) | async-done | bytes 3932192 | tf_op jit(solution)/shard_map/all_to_all | solution.py:21
  107.9 4.5 all-to-all-start.1
  115.6 24.9 %all-to-all-done.1 = bf16[16,48,1280]{2,1,0:T(8,128)(2,1)} async-done(((bf16[16,48,1280]{2,1,0:T(8,128)(2,1)}), bf16[16,48,1280]{2,1,0:T(8,128)(2,1)}, u32[]{:S(2)}, u32[]{:S(2)}) %all-to-all-start.1) | async-done | bytes 1966112 | tf_op jit(solution)/shard_map/all_to_all | solution.py:33
  140.5 4.1 reshape_reshape.3
  144.6 3.6 fusion.66
  149.3 5.3 %all-to-all-start.2 = ((bf16[8,192,320]{2,1,0:T(8,128)(2,1)}), bf16[8,192,320]{2,1,0:T(8,128)(2,1)S(1)}, u32[]{:S(2)}, u32[]{:S(2)}) async-start(bf16[8,192,320]{2,1,0:T(8,128)(2,1)} %broadcast_in_dim.158), calls=%async_computation.2 | async-start | bytes 2359296 | tf_op jit(solution)/shard_map/all_to_all | solution.py:33
  154.7 17.3 %all-to-all-done.2 = bf16[8,192,320]{2,1,0:T(8,128)(2,1)S(1)} async-done(((bf16[8,192,320]{2,1,0:T(8,128)(2,1)}), bf16[8,192,320]{2,1,0:T(8,128)(2,1)S(1)}, u32[]{:S(2)}, u32[]{:S(2)}) %all-to-all-start.2) | async-done | bytes 983072 | tf_op jit(solution)/shard_map/all_to_all | solution.py:33
  171.9 11.0 %gather_fusion = bf16[3072,320]{1,0:T(8,128)(2,1)S(1)} fusion(bf16[1536,320]{1,0:T(8,128)(2,1)S(1)} %bitcast.146, s32[3072]{0:T(1024)S(1)} %broadcast_clamp_fusion), kind=kCustom, calls=%fused_computation | custom fusion | bytes 3944448 | tf_op jit(solution)/shard_map/jit(_take)/gather | solution.py:151
  182.9 7.6 %fusion.47 = f32[3072,1024]{1,0:T(8,128)} fusion(bf16[320,1024]{1,0:T(8,128)(2,1)} %param.28, bf16[3072,320]{1,0:T(8,128)(2,1)S(1)} %gather_fusion, pred[3072]{0:T(1024)(128)(4,1)} %compare_and_fusion.1, pred[3072]{0:T(1024)(128)(4,1)S(1)} %ge.77), kind=kOutput, calls=%fused_computation.61 | convolution fusion | flops 2015232000 | bytes 15210496 | tf_op jit(solution)/shard_map/dot_general | solution.py:154
  192.2 88.8 %reduce-scatter.2.cloned.1.call-done = f32[192,1024]{1,0:T(8,128)} async-done(((f32[3072,1024]{1,0:T(8,128)}), f32[192,1024]{1,0:T(8,128)}) %reduce-scatter.2.cloned.1.call-update) | async-done | bytes 786448 | tf_op jit(solution)/shard_map/reduce_scatter | solution.py:153
  285.7 9.6 %all_to_all.21 = f32[8,1,384]{2,1,0:T(1,128)S(1)} all-to-all(f32[8,1,384]{2,1,0:T(1,128)S(1)} %broadcast_in_dim.162), channel_id=1, replica_groups=mesh['enc'=8,'ctx'=16] {'enc'}, dimensions={0} | all-to-all | bytes 24576 | tf_op jit(solution)/shard_map/all_to_all | solution.py:33
  295.3 30.6 %all-gather.3.cloned.1.call-done = bf16[384,8192]{1,0:T(8,128)(2,1)} async-done(((bf16[384,1024]{1,0:T(8,128)(2,1)}), bf16[384,8192]{1,0:T(8,128)(2,1)}) %all-gather.3.cloned.1.call-update) | async-done | bytes 6291472 | tf_op jit(solution)/shard_map/all_gather | solution.py:171
  325.9 5.7 %convolution_convert_fusion.2 = bf16[384,128]{0,1:T(8,128)(2,1)S(1)} fusion(bf16[8192,128]{1,0:T(8,128)(2,1)} %param.34, bf16[384,8192]{1,0:T(8,128)(2,1)} %all-gather.3.cloned.1.call-done, f32[8192]{0:T(1024)S(1)} %copy-done.10, f32[384]{0:T(512)S(1)} %add_rsqrt_fusion.1), kind=kOutput, calls=%fused_computation.76 | convolution fusion | flops 817938432 | bytes 8521216 | tf_op jit(solution)/shard_map/dot_general | solution.py:176
  338.5 8.7 %convolution_convert_fusion = bf16[384,512]{1,0:T(8,128)(2,1)S(1)} fusion(bf16[8192,512]{1,0:T(8,128)(2,1)} %param.33, bf16[384,8192]{1,0:T(8,128)(2,1)} %all-gather.3.cloned.1.call-done, f32[8192]{0:T(1024)S(1)} %copy-done.10, f32[384]{0:T(512)S(1)} %add_rsqrt_fusion.1), kind=kOutput, calls=%fused_computation.71 | convolution fusion | flops 3234004992 | bytes 15107584 | tf_op jit(solution)/shard_map/dot_general | solution.py:175
  348.1 38.2 %all-gather.5.cloned.1.call-done = bf16[6144,256]{0,1:T(8,128)(2,1)} async-done(((bf16[384,256]{0,1:T(8,128)(2,1)}), bf16[6144,256]{0,1:T(8,128)(2,1)}) %all-gather.5.cloned.1.call-update) | async-done | bytes 3145744 | tf_op jit(solution)/shard_map/all_gather | solution.py:47
  386.4 98.2 %conditional.1 = (f32[1,4,384]{2,1,0:T(4,128)}, f32[1,4,384,128]{3,2,1,0:T(8,128)}) conditional(s32[]{:T(128)} %convert_element_type.75, () %tuple.31, (bf16[6144,256]{0,1:T(8,128)(2,1)}, s32[]{:T(128)}, s32[384]{0:T(512)S(1)}, s32[6144]{0:T(1024)}, s32[384]{0:T(512)S(1)}, /*index=5*/bf16[1,4,384,128]{3,2,1,0:T(8,128)(2,1)}) %tuple.87), branch_computations={%region_17.18_spmd, %region_18.23_spmd} | conditional | flops 412493696 | bytes 25149788 | solution.py:238
  386.4 3.2 copy.44
  391.4 93.2 %while.27 = (s32[]{:T(128)}, f32[1,4,384]{2,1,0:T(4,128)S(1)}, f32[1,4,384]{2,1,0:T(4,128)}, f32[1,4,384,128]{3,2,1,0:T(8,128)}, s32[384]{0:T(512)S(1)}, /*index...) while((s32[]{:T(128)}, f32[1,4,384]{2,1,0:T(4,128)S(1)}, ...), condition=%wide.region_22.22_spmd.clone, body=%wide.region_19.21_spmd.clone.sunk | while | flops 412493312 | bytes 12563663 | solution.py:233
  408.9 3.1 fusion.116
  471.7 3.1 fusion.116
  479.5 3.1 fusion.116
  (219 shorter events, 129.9 us)
Async XLA Ops:
  6.5 138.1 %copy-start = (bf16[5120,320]{0,1:T(8,128)(2,1)S(1)}, bf16[5120,320]{0,1:T(8,128)(2,1)}, u32[]{:S(2)}) copy-start(bf16[5120,320]{0,1:T(8,128)(2,1)} %param.27) | copy-start | bytes 9830404
  6.5 3.0 copy-start.11
  6.5 2.3 copy-start.2
  6.5 3.0 copy-start.9
  9.5 5.7 %copy-start.6 = (s32[768]{0:T(1024)S(1)}, s32[768]{0:T(1024)}, u32[]{:S(2)}) copy-start(s32[768]{0:T(1024)} %param.22) | copy-start | bytes 9220
  36.0 66.7 %all-to-all-start = ((f32[16,48,1280]{2,1,0:T(8,128)}), f32[16,48,1280]{2,1,0:T(8,128)}, u32[]{:S(2)}, u32[]{:S(2)}) async-start(f32[16,48,1280]{2,1,0:T(8,128)} %fusion.79), calls=%async_computation | async-start | bytes 7864320 | tf_op jit(solution)/shard_map/all_to_all | solution.py:21
  43.2 63.2 %copy-start.5 = (f32[1280]{0:T(1024)S(1)}, f32[1280]{0:T(1024)}, u32[]{:S(2)}) copy-start(f32[1280]{0:T(1024)} %param.26) | copy-start | bytes 15364
  106.3 6.0 %copy-start.4 = (s32[6144]{0:T(1024)S(1)}, s32[6144]{0:T(1024)}, u32[]{:S(2)}) copy-start(s32[6144]{0:T(1024)} %param.30) | copy-start | bytes 73732
  107.9 32.7 %all-to-all-start.1 = ((bf16[16,48,1280]{2,1,0:T(8,128)(2,1)}), bf16[16,48,1280]{2,1,0:T(8,128)(2,1)}, u32[]{:S(2)}, u32[]{:S(2)}) async-start(bf16[16,48,1280]{2,1,0:T(8,128)(2,1)} %broadcast_in_dim.157), calls=%async_computation.1 | async-start | bytes 3932160 | tf_op jit(solution)/shard_map/all_to_all | solution.py:33
  149.3 22.6 %all-to-all-start.2 = ((bf16[8,192,320]{2,1,0:T(8,128)(2,1)}), bf16[8,192,320]{2,1,0:T(8,128)(2,1)S(1)}, u32[]{:S(2)}, u32[]{:S(2)}) async-start(bf16[8,192,320]{2,1,0:T(8,128)(2,1)} %broadcast_in_dim.158), calls=%async_computation.2 | async-start | bytes 2359296 | tf_op jit(solution)/shard_map/all_to_all | solution.py:33
  154.6 126.4 %reduce-scatter.2.cloned.1.call-start = ((), (), s32[]{:S(2)}) async-start(), calls=%async_computation.5 | async-start | bytes 13369344 | tf_op jit(solution)/shard_map/reduce_scatter | solution.py:153
  190.6 135.3 %all-gather.3.cloned.1.call-start = ((), (), s32[]{:S(2)}) async-start(), calls=%async_computation.6 | async-start | bytes 7077888 | tf_op jit(solution)/shard_map/all_gather | solution.py:171
  282.1 2.1 copy-start.3
  284.2 41.7 %copy-start.10 = (f32[8192]{0:T(1024)S(1)}, f32[8192]{0:T(1024)}, u32[]{:S(2)}) copy-start(f32[8192]{0:T(1024)} %param.32) | copy-start | bytes 98308
  285.6 100.7 %all-gather.5.cloned.1.call-start = ((), (), s32[]{:S(2)}) async-start(), calls=%async_computation.7 | async-start | bytes 3342336 | tf_op jit(solution)/shard_map/all_gather | solution.py:47
  295.3 36.3 %copy-start.8 = (bf16[8192,128]{1,0:T(8,128)(2,1)S(1)}, bf16[8192,128]{1,0:T(8,128)(2,1)}, u32[]{:S(2)}) copy-start(bf16[8192,128]{1,0:T(8,128)(2,1)} %param.35) | copy-start | bytes 6291460
  325.9 5.7 %copy-start.7 = (bf16[384,8192]{1,0:T(8,128)(2,1)S(1)}, bf16[384,8192]{1,0:T(8,128)(2,1)}, u32[]{:S(2)}) copy-start(bf16[384,8192]{1,0:T(8,128)(2,1)} %all-gather.3.cloned.1.call-done) | copy-start | bytes 18874372
  484.6 2.7 copy-start.1
Sparse Core Ops, SparseCore 0:
  190.7 90.2 reduce-scatter.1
  285.8 40.1 all-gather.2
  334.7 51.5 all-gather.4
where the time goes:
time: 496 us; the launch traced here: 494 us
  waiting for transfers between devices  259 us (52%)
  matrix products  97.8 us (20%)
  local copies, waits for them, and re-layouts  46.6 us (9%)
  other arithmetic  41.9 us (8%)
  starting transfers between devices  17.1 us (3%)
  between operations  14.8 us (3%)
  blocking collectives  9.58 us (2%)
  loops' own time  6.57 us (1%)
    reduce_scatter x1, waiting for transfers between devices, body(): lax.psum_scatter(jnp.dot(picked, merge_down, preferred_element_type=jnp.f...  88.8 us
    all_to_all x1, waiting for transfers between devices, sent_and_summed(): lax.all_to_all(blocks, axis, split_axis=0, concat_axis=0, tiled=True)  59.5 us
    all_to_all x2, waiting for transfers between devices, sent_to_all(): lax.all_to_all(jnp.broadcast_to(x[None], (size, *x.shape)), axis, 0, 0, t...  42.2 us
    all_gather x1, waiting for transfers between devices, in_one_piece(): result = lax.all_gather(both, axis, axis=dim, tiled=True)  38.2 us
    dot_general x12, matrix products, update_one_block(): jnp.einsum('gjts,sgd->gjtd', weights.astype(jnp.bfloat16), values_block,...  36.9 us
    all_gather x1, waiting for transfers between devices, body(): lax.all_gather(sequence, 'enc', axis=1, tiled=True).astype(jnp.float32)  30.6 us
    dot_general x12, matrix products, update_one_block(): jnp.einsum('gjtd,sgd->gjts', queries, keys_block, preferred_element_type=...  20.9 us
    add x12, other arithmetic, update_one_block(): totals = totals * factor + jnp.sum(weights, axis=3)  14.8 us
  transfers between devices with their start and end apart: 6, of which 6 were waited for; matrix products, arithmetic and copies ran while one was open for 3% of the time, Pallas kernels for 0%

commit v1 on v0

--- a/solution.py
+++ b/solution.py
@@ -168,7 +168,9 @@
         jnp.zeros((tok_rows, dec_wv.shape[1]), jnp.float32),
     )
     normed_part = (
-        lax.all_gather(sequence, "enc", axis=1, tiled=True).astype(jnp.float32)
+        jnp.concatenate(
+            lax.all_to_all(jnp.stack([sequence] * lax.axis_size("enc")), "enc", 0, 0), axis=1
+        ).astype(jnp.float32)
         * row_scale[:, None]
         * dec_gain
     ).astype(jnp.bfloat16)

time: 496 us -> 544 us (1.097)
  waiting for transfers between devices: 259 us -> 303 us
  blocking collectives: 9.58 us -> 0 us
  starting transfers between devices: 17.1 us -> 26.4 us
  local copies, waits for them, and re-layouts: 46.6 us -> 52.6 us
    all_to_all x0 -> x1, waiting for transfers between devices: none -> 72 us  [body(): lax.all_to_all(jnp.stack([sequence] * lax.axis_size('enc')), 'enc', 0, 0)]
    all_gather x1 -> x0, waiting for transfers between devices: 30.6 us -> none  [body(): lax.all_gather(sequence, 'enc', axis=1, tiled=True).astype(jnp.float32)]
    all_to_all x1 -> x0, blocking collectives: 9.58 us -> none  [sent_to_all(): lax.all_to_all(jnp.broadcast_to(x[None], (size, *x.shape)), axis, 0, 0, t...]
    all_to_all x2 -> x3, waiting for transfers between devices: 42.2 us -> 47.2 us  [sent_to_all(): lax.all_to_all(jnp.broadcast_to(x[None], (size, *x.shape)), axis, 0, 0, t...]
    all_to_all x2 -> x3, starting transfers between devices: 9.78 us -> 14.2 us  [sent_to_all(): lax.all_to_all(jnp.broadcast_to(x[None], (size, *x.shape)), axis, 0, 0, t...]
  transfers between devices with their start and end apart: 6 -> 7, of which waited for: 6 -> 7; matrix products, arithmetic and copies ran while one was open for 3% -> 3% of each run, Pallas kernels for 0% -> 0%
where the time goes in v1:
time: 544 us; the launch traced here: 541 us
  waiting for transfers between devices  303 us (56%)
  matrix products  92.7 us (17%)
  local copies, waits for them, and re-layouts  52.6 us (10%)
  other arithmetic  45.4 us (8%)
  starting transfers between devices  26.4 us (5%)
  between operations  15.1 us (3%)
  loops' own time  6.57 us (1%)
    reduce_scatter x1, waiting for transfers between devices, body(): lax.psum_scatter(jnp.dot(picked, merge_down, preferred_element_type=jnp.f...  88.8 us
    all_to_all x1, waiting for transfers between devices, body(): lax.all_to_all(jnp.stack([sequence] * lax.axis_size('enc')), 'enc', 0, 0)  72 us
    all_to_all x1, waiting for transfers between devices, sent_and_summed(): lax.all_to_all(blocks, axis, split_axis=0, concat_axis=0, tiled=True)  59.5 us
    all_to_all x3, waiting for transfers between devices, sent_to_all(): lax.all_to_all(jnp.broadcast_to(x[None], (size, *x.shape)), axis, 0, 0, t...  47.2 us
    dot_general x12, matrix products, update_one_block(): jnp.einsum('gjts,sgd->gjtd', weights.astype(jnp.bfloat16), values_block,...  36.9 us
    all_gather x1, waiting for transfers between devices, in_one_piece(): result = lax.all_gather(both, axis, axis=dim, tiled=True)  35.1 us
    dot_general x12, matrix products, update_one_block(): jnp.einsum('gjtd,sgd->gjts', queries, keys_block, preferred_element_type=...  20.9 us
    add x12, other arithmetic, update_one_block(): totals = totals * factor + jnp.sum(weights, axis=3)  14.8 us
  transfers between devices with their start and end apart: 7, of which 7 were waited for; matrix products, arithmetic and copies ran while one was open for 3% of the time, Pallas kernels for 0%

profile of v1, /device:TPU:0, one launch (start us, length us, event | category | flops | bytes accessed | tf_op | source)
XLA Modules:
  0.0 541.4 jit_solution(17789890437050249063)
XLA Ops:
  15.2 16.2 %while.28 = (s32[]{:T(128)}, bf16[3,1,256,80]{2,3,1,0:T(8,128)(2,1)}, s32[3]{0:T(128)S(1)}, s32[768]{0:T(1024)S(1)}, bf16[1,768,80]{2,1,0:T(8,128)(2,1)}, /*inde...) while((s32[]{:T(128)}, ...), condition=%wide.region_10.11_spmd, body=%wide.region_7.10_spmd.sunk | while | flops 64527876 | bytes 2797211 | solution.py:84
  32.5 3.5 fusion.81
  36.0 7.2 %all-to-all-start = ((f32[16,48,1280]{2,1,0:T(8,128)}), f32[16,48,1280]{2,1,0:T(8,128)}, u32[]{:S(2)}, u32[]{:S(2)}) async-start(f32[16,48,1280]{2,1,0:T(8,128)} %fusion.81), calls=%async_computation | async-start | bytes 7864320 | tf_op jit(solution)/shard_map/all_to_all | solution.py:21
  43.2 59.5 %all-to-all-done = f32[16,48,1280]{2,1,0:T(8,128)} async-done(((f32[16,48,1280]{2,1,0:T(8,128)}), f32[16,48,1280]{2,1,0:T(8,128)}, u32[]{:S(2)}, u32[]{:S(2)}) %all-to-all-start) | async-done | bytes 3932192 | tf_op jit(solution)/shard_map/all_to_all | solution.py:21
  107.9 4.5 all-to-all-start.1
  115.6 24.9 %all-to-all-done.1 = bf16[16,48,1280]{2,1,0:T(8,128)(2,1)} async-done(((bf16[16,48,1280]{2,1,0:T(8,128)(2,1)}), bf16[16,48,1280]{2,1,0:T(8,128)(2,1)}, u32[]{:S(2)}, u32[]{:S(2)}) %all-to-all-start.1) | async-done | bytes 1966112 | tf_op jit(solution)/shard_map/all_to_all | solution.py:33
  140.5 4.1 reshape_reshape.3
  144.6 3.6 fusion.68
  149.3 5.3 all-to-all-start.2
  154.7 17.3 %all-to-all-done.2 = bf16[8,192,320]{2,1,0:T(8,128)(2,1)S(1)} async-done(((bf16[8,192,320]{2,1,0:T(8,128)(2,1)}), bf16[8,192,320]{2,1,0:T(8,128)(2,1)S(1)}, u32[]{:S(2)}, u32[]{:S(2)}) %all-to-all-start.2) | async-done | bytes 983072 | tf_op jit(solution)/shard_map/all_to_all | solution.py:33
  171.9 11.0 %gather_fusion = bf16[3072,320]{1,0:T(8,128)(2,1)S(1)} fusion(bf16[1536,320]{1,0:T(8,128)(2,1)S(1)} %bitcast.157, s32[3072]{0:T(1024)S(1)} %broadcast_clamp_fusion), kind=kCustom, calls=%fused_computation | custom fusion | bytes 3944448 | tf_op jit(solution)/shard_map/jit(_take)/gather | solution.py:151
  182.9 7.6 %fusion.49 = f32[3072,1024]{1,0:T(8,128)} fusion(bf16[320,1024]{1,0:T(8,128)(2,1)} %param.28, bf16[3072,320]{1,0:T(8,128)(2,1)S(1)} %gather_fusion, pred[3072]{0:T(1024)(128)(4,1)} %compare_and_fusion.1, pred[3072]{0:T(1024)(128)(4,1)S(1)} %ge.77), kind=kOutput, calls=%fused_computation.63 | convolution fusion | flops 2015232000 | bytes 15210496 | tf_op jit(solution)/shard_map/dot_general | solution.py:154
  192.1 88.8 %reduce-scatter.2.cloned.1.call-done = f32[192,1024]{1,0:T(8,128)} async-done(((f32[3072,1024]{1,0:T(8,128)}), f32[192,1024]{1,0:T(8,128)}) %reduce-scatter.2.cloned.1.call-update) | async-done | bytes 786448 | tf_op jit(solution)/shard_map/reduce_scatter | solution.py:153
  285.4 4.4 all-to-all-start.4
  290.2 5.0 all-to-all-done.4
  295.1 3.2 stack.2
  298.3 4.9 all-to-all-start.3
  303.3 72.0 %all-to-all-done.3 = bf16[8,384,1024]{1,2,0:T(8,128)(2,1)} async-done(((bf16[8,384,1024]{1,2,0:T(8,128)(2,1)}), bf16[8,384,1024]{1,2,0:T(8,128)(2,1)}, u32[]{:S(2)}, u32[]{:S(2)}) %all-to-all-start.3) | async-done | bytes 6291488 | tf_op jit(solution)/shard_map/all_to_all | solution.py:172
  375.3 4.3 fusion.42
  388.8 8.8 %convolution_convert_fusion = bf16[384,512]{1,0:T(8,128)(2,1)S(1)} fusion(bf16[384,8192]{0,1:T(8,128)(2,1)} %copy-done.2, bf16[8192,512]{1,0:T(8,128)(2,1)} %param.33), kind=kOutput, calls=%fused_computation.73 | convolution fusion | flops 3221422080 | bytes 15073280 | tf_op jit(solution)/shard_map/dot_general | solution.py:177
  398.5 35.1 %all-gather.2.cloned.1.call-done = bf16[6144,256]{0,1:T(8,128)(2,1)} async-done(((bf16[384,256]{0,1:T(8,128)(2,1)}), bf16[6144,256]{0,1:T(8,128)(2,1)}) %all-gather.2.cloned.1.call-update) | async-done | bytes 3145744 | tf_op jit(solution)/shard_map/all_gather | solution.py:47
  433.6 98.2 %conditional.1 = (f32[1,4,384]{2,1,0:T(4,128)}, f32[1,4,384,128]{3,2,1,0:T(8,128)}) conditional(s32[]{:T(128)} %convert_element_type.81, () %tuple.31, (bf16[6144,256]{0,1:T(8,128)(2,1)}, s32[]{:T(128)}, s32[384]{0:T(512)S(1)}, s32[6144]{0:T(1024)}, s32[384]{0:T(512)S(1)}, /*index=5*/bf16[1,4,384,128]{3,2,1,0:T(8,128)(2,1)}) %tuple.85), branch_computations={%region_17.18_spmd, %region_18.23_spmd} | conditional | flops 412493696 | bytes 25149788 | solution.py:240
  433.6 3.2 copy.47
  438.7 93.2 %while.27 = (s32[]{:T(128)}, f32[1,4,384]{2,1,0:T(4,128)S(1)}, f32[1,4,384]{2,1,0:T(4,128)}, f32[1,4,384,128]{3,2,1,0:T(8,128)}, s32[384]{0:T(512)S(1)}, /*index...) while((s32[]{:T(128)}, f32[1,4,384]{2,1,0:T(4,128)S(1)}, ...), condition=%wide.region_22.22_spmd.clone, body=%wide.region_19.21_spmd.clone.sunk | while | flops 412493312 | bytes 12563663 | solution.py:235
  (224 shorter events, 141.6 us)
Async XLA Ops:
  6.5 138.1 %copy-start = (bf16[5120,320]{0,1:T(8,128)(2,1)S(1)}, bf16[5120,320]{0,1:T(8,128)(2,1)}, u32[]{:S(2)}) copy-start(bf16[5120,320]{0,1:T(8,128)(2,1)} %param.27) | copy-start | bytes 9830404
  6.5 3.0 copy-start.12
  6.5 2.3 copy-start.3
  6.5 3.0 copy-start.11
  9.5 5.7 %copy-start.8 = (s32[768]{0:T(1024)S(1)}, s32[768]{0:T(1024)}, u32[]{:S(2)}) copy-start(s32[768]{0:T(1024)} %param.22) | copy-start | bytes 9220
  36.0 66.7 %all-to-all-start = ((f32[16,48,1280]{2,1,0:T(8,128)}), f32[16,48,1280]{2,1,0:T(8,128)}, u32[]{:S(2)}, u32[]{:S(2)}) async-start(f32[16,48,1280]{2,1,0:T(8,128)} %fusion.81), calls=%async_computation | async-start | bytes 7864320 | tf_op jit(solution)/shard_map/all_to_all | solution.py:21
  43.2 63.2 %copy-start.7 = (f32[1280]{0:T(1024)S(1)}, f32[1280]{0:T(1024)}, u32[]{:S(2)}) copy-start(f32[1280]{0:T(1024)} %param.26) | copy-start | bytes 15364
  106.3 6.0 %copy-start.5 = (s32[6144]{0:T(1024)S(1)}, s32[6144]{0:T(1024)}, u32[]{:S(2)}) copy-start(s32[6144]{0:T(1024)} %param.30) | copy-start | bytes 73732
  107.9 32.7 %all-to-all-start.1 = ((bf16[16,48,1280]{2,1,0:T(8,128)(2,1)}), bf16[16,48,1280]{2,1,0:T(8,128)(2,1)}, u32[]{:S(2)}, u32[]{:S(2)}) async-start(bf16[16,48,1280]{2,1,0:T(8,128)(2,1)} %broadcast_in_dim.157), calls=%async_computation.1 | async-start | bytes 3932160 | tf_op jit(solution)/shard_map/all_to_all | solution.py:33
  149.3 22.6 %all-to-all-start.2 = ((bf16[8,192,320]{2,1,0:T(8,128)(2,1)}), bf16[8,192,320]{2,1,0:T(8,128)(2,1)S(1)}, u32[]{:S(2)}, u32[]{:S(2)}) async-start(bf16[8,192,320]{2,1,0:T(8,128)(2,1)} %broadcast_in_dim.158), calls=%async_computation.2 | async-start | bytes 2359296 | tf_op jit(solution)/shard_map/all_to_all | solution.py:33
  154.6 126.3 %reduce-scatter.2.cloned.1.call-start = ((), (), s32[]{:S(2)}) async-start(), calls=%async_computation.6 | async-start | bytes 13369344 | tf_op jit(solution)/shard_map/reduce_scatter | solution.py:153
  282.1 2.1 copy-start.4
  285.4 9.8 %all-to-all-start.4 = ((f32[8,1,384]{2,1,0:T(1,128)}), f32[8,1,384]{2,1,0:T(1,128)S(1)}, u32[]{:S(2)}, u32[]{:S(2)}) async-start(f32[8,1,384]{2,1,0:T(1,128)} %broadcast_in_dim.162), calls=%async_computation.5 | async-start | bytes 24576 | tf_op jit(solution)/shard_map/all_to_all | solution.py:33
  298.3 77.0 %copy-start.6 = (f32[8192]{0:T(1024)S(1)}, f32[8192]{0:T(1024)}, u32[]{:S(2)}) copy-start(f32[8192]{0:T(1024)} %param.32) | copy-start | bytes 98308
  298.3 77.0 %all-to-all-start.3 = ((bf16[8,384,1024]{1,2,0:T(8,128)(2,1)}), bf16[8,384,1024]{1,2,0:T(8,128)(2,1)}, u32[]{:S(2)}, u32[]{:S(2)}) async-start(bf16[8,384,1024]{1,2,0:T(8,128)(2,1)} %stack.2), calls=%async_computation.4 | async-start | bytes 12582912 | tf_op jit(solution)/shard_map/all_to_all | solution.py:172
  303.2 130.4 %all-gather.2.cloned.1.call-start = ((), (), s32[]{:S(2)}) async-start(), calls=%async_computation.7 | async-start | bytes 3342336 | tf_op jit(solution)/shard_map/all_gather | solution.py:47
  303.3 76.3 %copy-start.9 = (bf16[8192,128]{1,0:T(8,128)(2,1)S(1)}, bf16[8192,128]{1,0:T(8,128)(2,1)}, u32[]{:S(2)}) copy-start(bf16[8192,128]{1,0:T(8,128)(2,1)} %param.35) | copy-start | bytes 6291460
  379.6 2.9 copy-start.2
  379.6 3.2 copy-start.10
  531.8 2.7 copy-start.1
Sparse Core Ops, SparseCore 0:
  190.7 90.1 reduce-scatter.1
  384.9 48.6 all-gather.1
